TPU v7x, 256 devices: a whole 4x4x8 slice. The times are simulated.
256 devices in a mesh: fsdp: 16 (over z, y_hi), cols: 16 (over y_lo, x, core).
Axes of the slice: x: 4, y: 4 (y_hi: 2, y_lo: 2; y = y_hi * 2 + y_lo), z: 8, core: 2. Of those that a mesh axis runs over, the one named last changes fastest.
Arguments:
- train_gate: bfloat16 [3584, 14336], P('fsdp', 'cols'), may hold values from -0.09375 to 0.09375
- low_gate: bfloat16 [3584, 16], P('fsdp'), may hold values from -0.09375 to 0.09375
- high_gate: bfloat16 [16, 14336], P(None, 'cols'), may hold values from -1.5 to 1.5
- train_up: bfloat16 [3584, 14336], P('fsdp', 'cols'), may hold values from -0.09375 to 0.09375
- low_up: bfloat16 [3584, 16], P('fsdp'), may hold values from -0.09375 to 0.09375
- high_up: bfloat16 [16, 14336], P(None, 'cols'), may hold values from -1.5 to 1.5
- train_down: bfloat16 [14336, 3584], P('cols', 'fsdp'), may hold values from -0.046875 to 0.046875
- low_down: bfloat16 [14336, 16], P('cols'), may hold values from -0.046875 to 0.046875
- high_down: bfloat16 [16, 3584], P(None, 'fsdp'), may hold values from -1.5 to 1.5
- norm_train: float32 [3584], P(('fsdp', 'cols')), may hold values from 0.25 to 1.75
- norm_step: float32 [3584], P(('fsdp', 'cols')), may hold values from -0.3 to 0.3
Outputs:
- serving_gate: bfloat16 [3584, 14336], P(None, 'cols')
- serving_up: bfloat16 [3584, 14336], P(None, 'cols')
- serving_down: bfloat16 [14336, 3584], P('cols')
- serve_norm: bfloat16 [3584], replicated
All inputs are finite; a program needn't handle non-finite values.
Results may differ from a plain program's by a relative error of at most 0.001.
Values may be sent and summed in bfloat16 or wider, within the bound.
No kernel may reach another device: no remote copies, remote signals or barrier semaphores. Data moves between devices by JAX's collectives and lax.ppermute only.
A program may use at most 128 MiB of HBM per device.

v0:
```python
import jax
import jax.numpy as jnp
from jax import lax
from jax.sharding import PartitionSpec as P

mix_rate = 1.0


def rows_first(arrays, axis, dims):
    turned = [jnp.moveaxis(a, dim, 0) for a, dim in zip(arrays, dims)]
    both = jnp.concatenate([t.reshape(len(t), -1) for t in turned], axis=1)
    out, at, outs = (lax.all_gather(both, axis, axis=0, tiled=True), 0, [])
    for t, dim in zip(turned, dims):
        slab = out[:, at : at + t[0].size].reshape(-1, *t.shape[1:])
        outs.append(jnp.moveaxis(slab, 0, dim))
        at += t[0].size
    return tuple(outs)


def per_device(
    train_gate,
    low_gate,
    high_gate,
    train_up,
    low_up,
    high_up,
    train_down,
    low_down,
    high_down,
    norm_train,
    norm_step,
):
    whole_gate = train_gate.astype(jnp.float32) + mix_rate * jnp.dot(
        low_gate, high_gate, preferred_element_type=jnp.float32
    )
    whole_up = train_up.astype(jnp.float32) + mix_rate * jnp.dot(
        low_up, high_up, preferred_element_type=jnp.float32
    )
    whole_down = train_down.astype(jnp.float32) + mix_rate * jnp.dot(
        low_down, high_down, preferred_element_type=jnp.float32
    )
    narrow_gate, narrow_up, narrow_down = (
        whole_gate.astype(jnp.bfloat16),
        whole_up.astype(jnp.bfloat16),
        whole_down.astype(jnp.bfloat16),
    )
    serving_gate, serving_up, serving_down = rows_first(
        (narrow_gate, narrow_up, narrow_down), "fsdp", (0, 0, 1)
    )
    serve_norm = lax.all_gather(
        (norm_train + norm_step).astype(jnp.bfloat16), ("fsdp", "cols"), axis=0, tiled=True
    )
    return (serving_gate, serving_up, serving_down, serve_norm)


def solution(mesh):
    return jax.shard_map(
        per_device,
        mesh=mesh,
        in_specs=(
            P("fsdp", "cols"),
            P("fsdp", None),
            P(None, "cols"),
            P("fsdp", "cols"),
            P("fsdp", None),
            P(None, "cols"),
            P("cols", "fsdp"),
            P("cols", None),
            P(None, "fsdp"),
            P(("fsdp", "cols")),
            P(("fsdp", "cols")),
        ),
        out_specs=(P(None, "cols"), P(None, "cols"), P("cols", None), P()),
        check_vma=False,
    )
```

profile of v0, /device:TPU:1, one launch (start us, length us, event | category | flops | bytes accessed | tf_op | source)
XLA Modules:
  0.0 301.7 jit_solution(67208381330792148)
XLA Ops:
  7.2 0.0 copy-start
  7.2 0.0 all-gather.2.cloned.1.call-start
  7.2 0.7 copy-done
  7.9 1.3 fusion
  9.2 1.3 fusion.1
  10.6 0.0 copy-start.1
  10.6 0.0 copy-start.2
  10.6 1.4 fusion.3
  12.0 1.1 pad_maximum_fusion
  13.1 0.0 all-gather.2.cloned.1.call-update
  13.1 0.0 copy-done.1
  13.1 0.0 copy-done.2
  13.1 0.2 dynamic-update-slice
  13.4 189.9 %all-reduce = bf16[3584]{0:T(1024)(128)(2,1)} all-reduce(bf16[3584]{0:T(1024)(128)(2,1)S(1)} %dynamic-update-slice), channel_id=1, replica_groups=mesh['fsdp'=16,'cols'=16] {'fsdp','cols'}, use_global_device_ids=true, to_apply=%add | all-reduce | flops 3584 | bytes 14336
  203.3 67.5 %all-gather.2.cloned.1.call-done = bf16[3584,2688]{1,0:T(8,128)(2,1)} async-done(((bf16[224,2688]{1,0:T(8,128)(2,1)}), bf16[3584,2688]{1,0:T(8,128)(2,1)}) %all-gather.2.cloned.1.call-update) | async-done | bytes 19267600 | tf_op jit(solution)/shard_map/all_gather | solution.py:12
  270.8 14.6 %slice_bitcast_fusion = (bf16[896,3584]{0,1:T(8,128)(2,1)}, bf16[3584,896]{1,0:T(8,128)(2,1)}, bf16[3584,896]{1,0:T(8,128)(2,1)}) fusion(bf16[3584,2688]{1,0:T(8,128)(2,1)} %all-gather.2.cloned.1.call-done), kind=kLoop, calls=%fused_computation | loop fusion | bytes 38535168 | tf_op jit(solution)/shard_map/transpose | solution.py:15
  285.4 9.5 %copy.15 = bf16[896,3584]{1,0:T(8,128)(2,1)} copy(bf16[896,3584]{0,1:T(8,128)(2,1)} %get-tuple-element.8) | data formatting | bytes 12845056
  (2 shorter events, 0.0 us)
Async XLA Ops:
  7.2 0.8 copy-start
  7.2 263.6 %all-gather.2.cloned.1.call-start = ((), (), s32[]{:S(2)}) async-start(), calls=%async_computation | async-start | bytes 20471808 | tf_op jit(solution)/shard_map/all_gather | solution.py:12
  10.6 2.5 copy-start.1
  10.6 2.5 copy-start.2
Sparse Core Ops, SparseCore 0:
  13.2 257.5 all-gather.1
where the time goes:
time: 302 us
  blocking collectives  190 us (63%)
  waiting for transfers between devices  67.5 us (22%)
  local copies, waits for them, and re-layouts  25.1 us (8%)
  between operations  14.1 us (5%)
  matrix products  4 us (1%)
    unnamed x1, blocking collectives  190 us
    all_gather x1, waiting for transfers between devices, rows_first(): out, at, outs = (lax.all_gather(both, axis, axis=0, tiled=True), 0, [])  67.5 us
    transpose x1, local copies, waits for them, and re-layouts, rows_first(): outs.append(jnp.moveaxis(slab, 0, dim))  14.6 us
    unnamed x9, local copies, waits for them, and re-layouts  10.5 us
  transfers between devices with their start and end apart: 1, of which 1 were waited for; matrix products, arithmetic and copies ran while one was open for 0% of the time, Pallas kernels for 0%

commit v1 on v0

--- a/solution.py
+++ b/solution.py
@@ -9,7 +9,13 @@
 def rows_first(arrays, axis, dims):
     turned = [jnp.moveaxis(a, dim, 0) for a, dim in zip(arrays, dims)]
     both = jnp.concatenate([t.reshape(len(t), -1) for t in turned], axis=1)
-    out, at, outs = (lax.all_gather(both, axis, axis=0, tiled=True), 0, [])
+    out, at, outs = (
+        jnp.concatenate(
+            lax.all_to_all(jnp.stack([both] * lax.axis_size(axis)), axis, 0, 0), axis=0
+        ),
+        0,
+        [],
+    )
     for t, dim in zip(turned, dims):
         slab = out[:, at : at + t[0].size].reshape(-1, *t.shape[1:])
         outs.append(jnp.moveaxis(slab, 0, dim))

time: 302 us -> 534 us (1.77)
  blocking collectives: 190 us -> 485 us
  waiting for transfers between devices: 67.5 us -> 0.01 us
  between operations: 14.1 us -> 0.72 us
  starting transfers between devices: 0.04 us -> 11.9 us
  local copies, waits for them, and re-layouts: 25.1 us -> 31.8 us
    unnamed x1, blocking collectives: 190 us -> 485 us
    all_gather x1 -> x0, waiting for transfers between devices: 67.5 us -> none  [rows_first(): out, at, outs = (lax.all_gather(both, axis, axis=0, tiled=True), 0, [])]
    all_to_all x0 -> x1, starting transfers between devices: none -> 11.9 us  [rows_first(): lax.all_to_all(jnp.stack([both] * lax.axis_size(axis)), axis, 0, 0)]
    another operation x0 -> x1, local copies, waits for them, and re-layouts: none -> 6.71 us  [rows_first(): jnp.stack([both] * lax.axis_size(axis))]
  transfers between devices with their start and end apart: 1 -> 1, of which waited for: 1 -> 0; matrix products, arithmetic and copies ran while one was open for 0% -> 0% of each run, Pallas kernels for 0% -> 0%
where the time goes in v1:
time: 534 us; the launch traced here: 533 us
  blocking collectives  485 us (91%)
  local copies, waits for them, and re-layouts  31.8 us (6%)
  starting transfers between devices  11.9 us (2%)
    unnamed x1, blocking collectives  485 us
    transpose x1, local copies, waits for them, and re-layouts, rows_first(): outs.append(jnp.moveaxis(slab, 0, dim))  14.6 us
    all_to_all x1, starting transfers between devices, rows_first(): lax.all_to_all(jnp.stack([both] * lax.axis_size(axis)), axis, 0, 0)  11.9 us
  transfers between devices with their start and end apart: 1, of which 0 were waited for; matrix products, arithmetic and copies ran while one was open for 0% of the time, Pallas kernels for 0%

profile of v1, /device:TPU:1, one launch (start us, length us, event | category | flops | bytes accessed | tf_op | source)
XLA Modules:
  0.0 533.4 jit_solution(11799049675258787030)
XLA Ops:
  0.6 0.0 copy-start
  0.6 0.7 copy-done
  1.4 1.3 fusion
  2.7 1.3 fusion.1
  4.0 1.3 fusion.3
  5.4 0.1 pad_maximum_fusion
  5.5 6.7 %stack.2 = bf16[16,224,2688]{2,1,0:T(8,128)(2,1)} broadcast(bf16[224,2688]{1,0:T(8,128)(2,1)S(1)} %pad_maximum_fusion), dimensions={1,2} | broadcast | bytes 20471808 | tf_op jit(solution)/shard_map/stack | solution.py:14
  12.2 0.0 copy-start.2
  12.2 0.0 copy-start.3
  12.2 11.9 %all-to-all-start = ((bf16[16,224,2688]{2,1,0:T(8,128)(2,1)}), bf16[16,224,2688]{2,1,0:T(8,128)(2,1)}, u32[]{:S(2)}, u32[]{:S(2)}) async-start(bf16[16,224,2688]{2,1,0:T(8,128)(2,1)} %stack.2), calls=%async_computation | async-start | bytes 38535168 | tf_op jit(solution)/shard_map/all_to_all | solution.py:14
  24.1 0.0 copy-done.2
  24.2 0.0 copy-done.3
  24.2 0.2 dynamic-update-slice
  24.4 484.9 %all-reduce = bf16[3584]{0:T(1024)(128)(2,1)} all-reduce(bf16[3584]{0:T(1024)(128)(2,1)S(1)} %dynamic-update-slice), channel_id=1, replica_groups=mesh['fsdp'=16,'cols'=16] {'fsdp','cols'}, use_global_device_ids=true, to_apply=%add | all-reduce | flops 3584 | bytes 14336
  509.3 0.0 all-to-all-done
  509.3 14.6 %slice_bitcast_fusion = (bf16[896,3584]{0,1:T(8,128)(2,1)}, bf16[3584,896]{1,0:T(8,128)(2,1)}, bf16[3584,896]{1,0:T(8,128)(2,1)}) fusion(bf16[3584,2688]{1,0:T(8,128)(2,1)} %bitcast.1), kind=kLoop, calls=%fused_computation | loop fusion | bytes 38535168 | tf_op jit(solution)/shard_map/transpose | solution.py:21
  523.9 0.0 copy-start.1
  523.9 9.5 %copy.18 = bf16[896,3584]{1,0:T(8,128)(2,1)} copy(bf16[896,3584]{0,1:T(8,128)(2,1)} %get-tuple-element.12) | data formatting | bytes 12845056
  533.4 0.0 copy-done.1
  (2 shorter events, 0.0 us)
Async XLA Ops:
  0.6 0.8 copy-start
  12.2 11.9 %copy-start.2 = (f32[14]{0:T(128)S(1)}, f32[14]{0:T(128)}, u32[]{:S(2)}) copy-start(f32[14]{0:T(128)} %param.20) | copy-start | bytes 172
  12.2 11.9 %copy-start.3 = (f32[14]{0:T(128)S(1)}, f32[14]{0:T(128)}, u32[]{:S(2)}) copy-start(f32[14]{0:T(128)} %param.21) | copy-start | bytes 172
  12.2 497.1 %all-to-all-start = ((bf16[16,224,2688]{2,1,0:T(8,128)(2,1)}), bf16[16,224,2688]{2,1,0:T(8,128)(2,1)}, u32[]{:S(2)}, u32[]{:S(2)}) async-start(bf16[16,224,2688]{2,1,0:T(8,128)(2,1)} %stack.2), calls=%async_computation | async-start | bytes 38535168 | tf_op jit(solution)/shard_map/all_to_all | solution.py:14
  523.9 9.5 %copy-start.1 = (bf16[16,896]{1,0:T(8,128)(2,1)S(1)}, bf16[16,896]{1,0:T(8,128)(2,1)}, u32[]{:S(2)}) copy-start(bf16[16,896]{1,0:T(8,128)(2,1)} %param.13) | copy-start | bytes 86020
